TPU v7x, 32 devices: a whole 2x2x4 slice. The times are simulated.
32 devices in a mesh: fsdp: 16 (over z, y, x), dp: 2 (over core).
Axes of the slice: x: 2, y: 2, z: 4, core: 2. Of those that a mesh axis runs over, the one named last changes fastest.
Arguments:
- normed: bfloat16 [2, 4096, 4096], P(None, ('fsdp', 'dp')), may hold values from -6 to 6
- kv_cotangent: bfloat16 [2, 4096, 512], P(None, ('fsdp', 'dp')), may hold values from -6 to 6
- kv_weight: bfloat16 [4096, 512], P('fsdp'), may hold values from -0.09375 to 0.09375
- main_grad: float32 [4096, 512], P('fsdp'), may hold values from -6 to 6
- owner_order: int32 [16], replicated, may hold values from 0 to 15, each once
Outputs:
- key_rows: bfloat16 [2, 4096, 512], P(None, ('fsdp', 'dp'))
- input_grad: bfloat16 [2, 4096, 4096], P(None, ('fsdp', 'dp'))
- grad_buffer: float32 [4096, 512], P('fsdp')
Inputs may be any that keep to these rules, and one draw needn't show every extreme that they name: `owner_order`: a permutation: each value appears once.
All inputs are finite; a program needn't handle non-finite values.
Results may differ from a plain program's by a relative error of at most 0.0075.
Values may be sent and summed in bfloat16 or wider, within the bound.
A program may use at most 64 MiB of HBM per device.

v0:
```python
import math

import jax
import jax.numpy as jnp
from jax import lax
from jax.sharding import PartitionSpec as P


def term_from(inputs, cotangent):

    def gradient_term(first_row, row_count):
        return lax.dot_general(
            inputs, cotangent, (((0,), (0,)), ((), ())), preferred_element_type=jnp.float32
        )

    return gradient_term


def body(normed, kv_cotangent, kv_weight, main_grad, owner_order):
    micro_count, tok_dev, width = normed.shape
    shard_rows, key_width = kv_weight.shape
    owners = lax.axis_size("fsdp")
    everyone = owners * lax.axis_size("dp")
    all_rows = micro_count * tok_dev
    permuted = jnp.take(normed.reshape(all_rows, owners, shard_rows), owner_order, axis=1).reshape(
        all_rows, width
    )
    flat_cot = kv_cotangent.reshape(all_rows, key_width)
    gathered = lax.all_gather(kv_weight, "fsdp", axis=0, tiled=True)
    key_sum = jnp.dot(permuted, gathered, preferred_element_type=jnp.float32)
    grad_permuted = lax.dot_general(
        flat_cot, gathered, (((1,), (1,)), ((), ())), preferred_element_type=jnp.float32
    ).astype(jnp.bfloat16)
    indices = jnp.arange(owners, dtype=jnp.int32)
    inverse_owner = jnp.sum(
        jnp.where(owner_order[None, :] == indices[:, None], indices[None, :], 0), axis=1
    )
    input_grad = jnp.take(
        grad_permuted.reshape(all_rows, owners, shard_rows), inverse_owner, axis=1
    ).reshape(micro_count, tok_dev, width)
    shard_sum = jnp.zeros((shard_rows, key_width), jnp.float32)
    for micro_index in range(micro_count):
        lower = micro_index * tok_dev
        upper = lower + tok_dev
        gradient_term = term_from(permuted[lower:upper], flat_cot[lower:upper])
        shard_sum = shard_sum + lax.psum_scatter(
            gradient_term(jnp.int32(0), shard_rows * lax.axis_size("fsdp")),
            "fsdp",
            scatter_dimension=0,
            tiled=True,
        )
    replica_total = lax.psum(shard_sum.astype(jnp.bfloat16), "dp").astype(jnp.float32)
    grad_scale = 1.0 / math.sqrt(micro_count * tok_dev * everyone)
    grad_buffer = main_grad + replica_total * grad_scale
    key_rows = key_sum.astype(jnp.bfloat16).reshape(micro_count, tok_dev, key_width)
    return (key_rows, input_grad, grad_buffer)


def solution(mesh):
    in_specs = (
        P(None, ("fsdp", "dp"), None),
        P(None, ("fsdp", "dp"), None),
        P("fsdp", None),
        P("fsdp", None),
        P(),
    )
    out_specs = (P(None, ("fsdp", "dp"), None), P(None, ("fsdp", "dp"), None), P("fsdp", None))
    return jax.shard_map(body, mesh=mesh, in_specs=in_specs, out_specs=out_specs, check_vma=False)
```

profile of v0, /device:TPU:0, one launch (start us, length us, event | category | flops | bytes accessed | tf_op | source)
XLA Modules:
  0.0 299.8 jit_solution(3278835918470781926)
XLA Ops:
  7.2 0.7 all-gather.2.cloned.1.call-update
  7.9 2.2 copy.22
  10.2 0.7 copy.15
  10.9 2.0 gather_fusion
  12.9 1.8 select_bitcast_fusion.1
  14.8 1.5 fusion.5
  16.3 1.7 copy.19
  17.9 2.3 copy.20
  20.2 1.2 fusion.1
  21.5 4.5 %convolution_add_fusion = f32[4096,512]{1,0:T(8,128)} fusion(f32[4096,512]{1,0:T(8,128)S(1)} %fusion.1, bf16[128,4096]{0,1:T(8,128)(2,1)S(1)} %bitcast.32, bf16[2,128,512]{2,1,0:T(8,128)(2,1)S(1)} %copy-done.1), kind=kOutput, calls=%fused_computation.2 | convolution fusion | flops 538968064 | bytes 17956864 | tf_op jit(solution)/shard_map/dot_general | solution.py:12
  26.0 2.4 copy.16
  28.4 0.1 select_reduce_fusion
  28.6 60.5 %all-gather.2.cloned.1.call-done = bf16[4096,512]{1,0:T(8,128)(2,1)} async-done(((bf16[256,512]{1,0:T(8,128)(2,1)}), bf16[4096,512]{1,0:T(8,128)(2,1)}) %all-gather.2.cloned.1.call-update) | async-done | bytes 4194320 | tf_op jit(solution)/shard_map/all_gather | solution.py:29
  89.1 3.5 %convolution_convert_fusion = bf16[256,4096]{1,0:T(8,128)(2,1)S(1)} fusion(bf16[256,512]{1,0:T(8,128)(2,1)S(1)} %bitcast.35, bf16[4096,512]{1,0:T(8,128)(2,1)} %all-gather.2.cloned.1.call-done), kind=kOutput, calls=%fused_computation.3 | convolution fusion | flops 1074790400 | bytes 6553600 | tf_op jit(solution)/shard_map/dot_general | solution.py:31
  92.6 1.5 copy.24
  94.1 2.3 gather_fusion.1
  96.4 0.3 select_bitcast_fusion
  96.7 1.2 copy.18
  97.8 2.3 reshape.39
  100.2 167.7 %reduce-scatter.2.cloned.1.call-done = f32[256,512]{1,0:T(8,128)} async-done(((f32[4096,512]{1,0:T(8,128)}), f32[256,512]{1,0:T(8,128)}) %reduce-scatter.2.cloned.1.call-update) | async-done | bytes 524304 | tf_op jit(solution)/shard_map/reduce_scatter | solution.py:46
  267.9 1.8 convert_element_type.14
  269.7 4.8 %convolution_convert_fusion.1 = bf16[256,512]{1,0:T(8,128)(2,1)} fusion(bf16[256,4096]{0,1:T(8,128)(2,1)} %bitcast.34, bf16[4096,512]{1,0:T(8,128)(2,1)} %all-gather.2.cloned.1.call-done), kind=kOutput, calls=%fused_computation.7 | convolution fusion | flops 1073872896 | bytes 6553600 | tf_op jit(solution)/shard_map/dot_general | solution.py:30
  274.5 16.9 %all-reduce.2.cloned.1.call-done = bf16[256,512]{1,0:T(8,128)(2,1)} async-done(((bf16[256,512]{1,0:T(8,128)(2,1)}), bf16[256,512]{1,0:T(8,128)(2,1)}) %all-reduce.2.cloned.1.call-update) | async-done | bytes 262160 | tf_op jit(solution)/shard_map/psum | solution.py:52
  291.5 1.8 multiply_add_fusion
  (19 shorter events, 0.2 us)
Async XLA Ops:
  7.2 81.9 %all-gather.2.cloned.1.call-start = ((), (), s32[]{:S(2)}) async-start(), calls=%async_computation.1 | async-start | bytes 4456448 | tf_op jit(solution)/shard_map/all_gather | solution.py:29
  7.9 260.0 %reduce-scatter.2.cloned.1.call-start = ((), (), s32[]{:S(2)}) async-start(), calls=%async_computation.3 | async-start | bytes 8912896 | tf_op jit(solution)/shard_map/reduce_scatter | solution.py:46
  10.2 0.7 copy-start.3
  16.3 3.9 %copy-start.1 = (bf16[2,128,512]{2,1,0:T(8,128)(2,1)S(1)}, bf16[2,128,512]{2,1,0:T(8,128)(2,1)}, u32[]{:S(2)}) copy-start(bf16[2,128,512]{2,1,0:T(8,128)(2,1)} %param.8) | copy-start | bytes 786436
  20.2 1.3 copy-start
  25.9 265.5 %all-reduce.2.cloned.1.call-start = ((), (), s32[]{:S(2)}) async-start(), calls=%async_computation.2 | async-start | bytes 524288 | tf_op jit(solution)/shard_map/psum | solution.py:52
  269.7 21.8 %copy-start.2 = (f32[256,512]{1,0:T(8,128)S(1)}, f32[256,512]{1,0:T(8,128)}, u32[]{:S(2)}) copy-start(f32[256,512]{1,0:T(8,128)} %param.10) | copy-start | bytes 1572868
Sparse Core Ops, SparseCore 0:
  10.7 78.3 all-gather.1
  91.4 176.4 reduce-scatter.1
  270.8 20.6 all-reduce.1
where the time goes:
time: 300 us
  waiting for transfers between devices  246 us (82%)
  local copies, waits for them, and re-layouts  20.1 us (7%)
  matrix products  14 us (5%)
  between operations  13.9 us (5%)
  other arithmetic  5.86 us (2%)
    reduce_scatter x1, waiting for transfers between devices, body(): lax.psum_scatter(gradient_term(jnp.int32(0), shard_rows * lax.axis_size('...  168 us
    all_gather x1, waiting for transfers between devices, body(): gathered = lax.all_gather(kv_weight, 'fsdp', axis=0, tiled=True)  60.5 us
    psum x1, waiting for transfers between devices, body(): lax.psum(shard_sum.astype(jnp.bfloat16), 'dp').astype(jnp.float32)  16.9 us
  transfers between devices with their start and end apart: 3, of which 3 were waited for; matrix products, arithmetic and copies ran while one was open for 12% of the time, Pallas kernels for 0%

commit v1 on v0

v1 whole, which is shorter than its diff:
```python
import functools
import math

import jax
import jax.numpy as jnp
from jax import lax
from jax.experimental import pallas as pl
from jax.experimental.pallas import tpu as pltpu
from jax.sharding import PartitionSpec as P

MESH = pl.DeviceIdType.MESH
F32 = jnp.float32
BF16 = jnp.bfloat16


def kernel(
    n, dp, chunk, scale,
    x_hbm, c_hbm, w_hbm, main_hbm,
    key_hbm, ig_hbm, gb_hbm,
    xx, cc, ck, gath, part, r1, t1, r2, t2, r3, fin, main, gb, key, ig,
    load_sem, out_sem, send_sem, x_recv, az_recv, a1_recv, a2_recv, ad_recv, r1_recv, r2_recv, r3_recv, rd_recv,
):
    f = lax.axis_index("fsdp")
    d = lax.axis_index("dp")
    k = lax.rem(d, 2)
    sib = d + 1 - 2 * k
    rows, width = x_hbm.shape
    key_width = c_hbm.shape[1]
    half = key_width // 2
    depth = n // 4
    chunks = width // chunk
    z = lax.div(f, 4)
    low = lax.rem(f, 4)
    bit0 = lax.rem(low, 2)
    bit1 = lax.div(low, 2)
    flip_x = low + 1 - 2 * bit0
    flip_y = low + 2 - 4 * bit1
    low1 = flip_x + k * (flip_y - flip_x)
    low2 = flip_y + k * (flip_x - flip_y)
    low12 = 3 - low
    p1 = z * 4 + low1
    p2 = z * 4 + low2
    steps = sorted(range(1, depth), key=lambda s: (min(s, depth - s), s))

    def peer(s):
        return lax.rem(z + s, depth)

    def dev(fi, di):
        return {"fsdp": fi, "dp": di}

    loads = []

    def load(src, dst, i):
        cp = pltpu.make_async_copy(src, dst, load_sem.at[i])
        cp.start()
        loads.append(cp)

    load(w_hbm.at[:, pl.ds(0, half)], gath.at[0, f], 0)
    load(w_hbm.at[:, pl.ds(half, half)], gath.at[1, f], 1)
    load(c_hbm, cc.at[0], 2)
    load(x_hbm, xx.at[0], 3)
    load(main_hbm, main, 4)

    barrier = pltpu.get_barrier_semaphore()
    greeted = [dev(peer(s) * 4 + low, d) for s in steps]
    greeted += [dev(p1, d), dev(p2, d)]
    greeted += [dev(f, lax.rem(d + s, dp)) for s in range(1, dp)]
    for g in greeted:
        pl.semaphore_signal(barrier, inc=1, device_id=g, device_id_type=MESH)
    pl.semaphore_wait(barrier, len(greeted))

    sent = []

    def send(src, dst, rsem, to):
        cp = pltpu.make_async_remote_copy(
            src_ref=src, dst_ref=dst, send_sem=send_sem, recv_sem=rsem, device_id=to, device_id_type=MESH
        )
        cp.start()
        sent.append(cp)

    def arrived(dst, rsem, frm):
        pltpu.make_async_remote_copy(
            src_ref=dst, dst_ref=dst, send_sem=send_sem, recv_sem=rsem, device_id=frm, device_id_type=MESH
        ).wait_recv()

    to_sib = dev(f, sib)
    to1 = dev(p1, d)
    to2 = dev(p2, d)

    send(x_hbm, xx.at[1], x_recv.at[0], to_sib)
    send(c_hbm, cc.at[1], x_recv.at[1], to_sib)
    loads[0].wait()
    loads[1].wait()

    def block(fi):
        return gath.at[k, fi]

    send(block(f), block(f), a1_recv.at[z], to1)
    send(block(f), block(f), a2_recv.at[z], to2)
    for s in steps:
        send(block(f), block(f), az_recv.at[z], dev(peer(s) * 4 + low, d))

    loads[2].wait()
    loads[3].wait()
    arrived(cc.at[1], x_recv.at[1], to_sib)
    arrived(xx.at[1], x_recv.at[0], to_sib)
    side = pl.ds(pl.multiple_of(k * half, half), half)
    ck[...] = cc[:, :, side].reshape(2 * rows, half)

    per = chunk // part.shape[1]
    for j in range(chunks):
        both = xx[:, :, j * chunk : (j + 1) * chunk].reshape(2 * rows, chunk)
        prod = lax.dot_general(both, ck[...], (((0,), (0,)), ((), ())), preferred_element_type=F32)
        part[j * per : (j + 1) * per] = prod.astype(BF16).reshape(per, part.shape[1], half)

    ring = steps + [0]
    for s in ring:
        send(part.at[peer(s) * 4 + low12], r1.at[0, peer(s)], r1_recv.at[0, peer(s)], to1)
    for s in steps:
        zb = peer(s)
        fb = zb * 4 + low
        arrived(block(fb), az_recv.at[zb], dev(fb, d))
        send(block(fb), block(fb), a1_recv.at[zb], to1)
        send(block(fb), block(fb), a2_recv.at[zb], to2)
        send(block(fb), block(fb), ad_recv.at[fb], to_sib)
    for s in ring:
        send(part.at[peer(s) * 4 + low1], r1.at[1, peer(s)], r1_recv.at[1, peer(s)], to1)
    for s in [0] + steps:
        zb = peer(s)
        fb = zb * 4 + low1
        arrived(block(fb), a1_recv.at[zb], to1)
        send(block(fb), block(fb), a2_recv.at[depth + zb], to2)
        send(block(fb), block(fb), ad_recv.at[fb], to_sib)
    for s in ring:
        zb = peer(s)
        arrived(r1.at[0, zb], r1_recv.at[0, zb], to1)
        t1[zb] = (part[zb * 4 + low2].astype(F32) + r1[0, zb].astype(F32)).astype(BF16)
        send(t1.at[zb], r2.at[zb], r2_recv.at[zb], to2)
    for s in steps:
        zb = peer(s)
        arrived(r1.at[1, zb], r1_recv.at[1, zb], to1)
        arrived(r2.at[zb], r2_recv.at[zb], to2)
        t2[zb] = (part[zb * 4 + low].astype(F32) + r1[1, zb].astype(F32) + r2[zb].astype(F32)).astype(BF16)
        send(t2.at[zb], r3.at[z], r3_recv.at[z], dev(zb * 4 + low, d))
    for s in [0] + steps:
        zb = peer(s)
        fb = zb * 4 + low2
        arrived(block(fb), a2_recv.at[zb], to2)
        send(block(fb), block(fb), ad_recv.at[fb], to_sib)
    for s in [0] + steps:
        zb = peer(s)
        fb = zb * 4 + low12
        arrived(block(fb), a2_recv.at[depth + zb], to2)
        send(block(fb), block(fb), ad_recv.at[fb], to_sib)

    arrived(r1.at[1, z], r1_recv.at[1, z], to1)
    arrived(r2.at[z], r2_recv.at[z], to2)
    total = part[f].astype(F32) + r1[1, z].astype(F32) + r2[z].astype(F32)
    for s in steps:
        arrived(r3.at[peer(s)], r3_recv.at[peer(s)], dev(peer(s) * 4 + low, d))
        total = total + r3[peer(s)].astype(F32)
    fin[d] = total
    for s in range(1, dp):
        send(fin.at[d], fin.at[d], rd_recv.at[d], dev(f, lax.rem(d + s, dp)))

    for s in [0] + steps:
        for lo in (low, low1, low2, low12):
            if s == 0 and lo is low:
                continue
            fb = peer(s) * 4 + lo
            arrived(gath.at[1 - k, fb], ad_recv.at[fb], to_sib)

    outs = []

    def put(src, dst, i):
        cp = pltpu.make_async_copy(src, dst, out_sem.at[i])
        cp.start()
        outs.append(cp)

    group = max(1, chunks // 4)
    for j in range(chunks):
        w0 = gath[0, j * per : (j + 1) * per].reshape(chunk, half)
        w1 = gath[1, j * per : (j + 1) * per].reshape(chunk, half)
        contract = (((1,), (1,)), ((), ()))
        prod = lax.dot_general(cc[0, :, :half], w0, contract, preferred_element_type=F32)
        prod = prod + lax.dot_general(cc[0, :, half:], w1, contract, preferred_element_type=F32)
        ig[:, j * chunk : (j + 1) * chunk] = prod.astype(BF16)
        if (j + 1) % group == 0:
            cols = pl.ds((j + 1 - group) * chunk, group * chunk)
            put(ig.at[:, cols], ig_hbm.at[:, cols], (j + 1) // group - 1)
    for h in range(2):
        w = gath[h].reshape(width, half)
        key[:, h * half : (h + 1) * half] = jnp.dot(xx[0], w, preferred_element_type=F32).astype(BF16)
    put(key, key_hbm, chunks // group)

    for s in range(1, dp):
        src = lax.rem(d + s, dp)
        arrived(fin.at[src], rd_recv.at[src], dev(f, src))
    loads[4].wait()
    for h in range(2):
        total = fin[h]
        for g in range(1, dp // 2):
            total = total + fin[2 * g + h]
        cols = slice(h * half, (h + 1) * half)
        gb[:, cols] = main[:, cols] + total * scale
    put(gb, gb_hbm, chunks // group + 1)
    for cp in sent:
        cp.wait_send()
    for cp in outs:
        cp.wait()


def reorder_kernel(depth, scatter, order_ref, x_ref, y_ref):
    for j in range(x_ref.shape[1] // depth):
        here = slice(j * depth, (j + 1) * depth)
        there = pl.ds(pl.multiple_of(order_ref[j] * depth, depth), depth)
        if scatter:
            y_ref[:, there] = x_ref[:, here]
        else:
            y_ref[:, here] = x_ref[:, there]


def reorder(x, order, scatter):
    rows, width = x.shape
    n = order.shape[0]
    depth = width // n
    if depth % 128:
        if scatter:
            order = jnp.argsort(order)
        return jnp.take(x.reshape(rows, n, depth), order, axis=1, mode="clip").reshape(rows, width)
    tile = rows // 4
    spec = pl.BlockSpec((tile, width), lambda i: (i, 0))
    return pl.pallas_call(
        functools.partial(reorder_kernel, depth, scatter),
        grid=(rows // tile,),
        out_shape=jax.ShapeDtypeStruct((rows, width), x.dtype),
        in_specs=[pl.BlockSpec(memory_space=pltpu.SMEM), spec],
        out_specs=spec,
        cost_estimate=pl.CostEstimate(flops=0, bytes_accessed=4 * rows * width, transcendentals=0),
    )(order, x)


def body(normed, kv_cotangent, kv_weight, main_grad, owner_order):
    micro_count, tok_dev, width = normed.shape
    shard_rows, key_width = kv_weight.shape
    n = lax.axis_size("fsdp")
    dp = lax.axis_size("dp")
    rows = micro_count * tok_dev
    half = key_width // 2
    depth = n // 4
    scale = 1.0 / math.sqrt(rows * n * dp)
    chunk = max(shard_rows, 256)
    x = reorder(normed.reshape(rows, width), owner_order, False)
    chunks = width // chunk
    dma = pltpu.SemaphoreType.DMA
    half_block = (shard_rows, half)
    any_spec = pl.BlockSpec(memory_space=pl.ANY)
    key, ig, gb = pl.pallas_call(
        functools.partial(kernel, n, dp, chunk, scale),
        out_shape=(
            jax.ShapeDtypeStruct((rows, key_width), BF16),
            jax.ShapeDtypeStruct((rows, width), BF16),
            jax.ShapeDtypeStruct((shard_rows, key_width), F32),
        ),
        in_specs=[any_spec] * 4,
        out_specs=(any_spec,) * 3,
        scratch_shapes=[
            pltpu.VMEM((2, rows, width), BF16),
            pltpu.VMEM((2, rows, key_width), BF16),
            pltpu.VMEM((2 * rows, half), BF16),
            pltpu.VMEM((2, n) + half_block, BF16),
            pltpu.VMEM((n,) + half_block, BF16),
            pltpu.VMEM((2, depth) + half_block, BF16),
            pltpu.VMEM((depth,) + half_block, BF16),
            pltpu.VMEM((depth,) + half_block, BF16),
            pltpu.VMEM((depth,) + half_block, BF16),
            pltpu.VMEM((depth,) + half_block, BF16),
            pltpu.VMEM((dp,) + half_block, F32),
            pltpu.VMEM((shard_rows, key_width), F32),
            pltpu.VMEM((shard_rows, key_width), F32),
            pltpu.VMEM((rows, key_width), BF16),
            pltpu.VMEM((rows, width), BF16),
            dma((5,)),
            dma((chunks // max(1, chunks // 4) + 2,)),
            dma,
            dma((2,)),
            dma((depth,)),
            dma((depth,)),
            dma((2 * depth,)),
            dma((n,)),
            dma((2, depth)),
            dma((depth,)),
            dma((depth,)),
            dma((dp,)),
        ],
        compiler_params=pltpu.CompilerParams(
            collective_id=0, has_side_effects=True
        ),
    )(x, kv_cotangent.reshape(rows, key_width), kv_weight, main_grad)
    ig = reorder(ig, owner_order, True)
    return (
        key.reshape(micro_count, tok_dev, key_width),
        ig.reshape(micro_count, tok_dev, width),
        gb,
    )


def solution(mesh):
    in_specs = (
        P(None, ("fsdp", "dp"), None),
        P(None, ("fsdp", "dp"), None),
        P("fsdp", None),
        P("fsdp", None),
        P(),
    )
    out_specs = (P(None, ("fsdp", "dp"), None), P(None, ("fsdp", "dp"), None), P("fsdp", None))
    return jax.shard_map(body, mesh=mesh, in_specs=in_specs, out_specs=out_specs, check_vma=False)
```

time: 300 us -> 66.4 us (0.22)
  waiting for transfers between devices: 246 us -> 0 us
  Pallas kernels: 0 us -> 64 us
  local copies, waits for them, and re-layouts: 20.1 us -> 1.5 us
  matrix products: 14 us -> 0 us
  between operations: 13.9 us -> 0.66 us
  other arithmetic: 5.86 us -> 0 us
    reduce_scatter x1 -> x0, waiting for transfers between devices: 168 us -> none  [body(): lax.psum_scatter(gradient_term(jnp.int32(0), shard_rows * lax.axis_size('...]
    pallas_call x0 -> x3, Pallas kernels: none -> 64 us  [the longest x1 56.2 us: body(): pl.pallas_call(functools.partial(kernel, n, dp, chunk, scale), out_shape=...]
    all_gather x1 -> x0, waiting for transfers between devices: 60.5 us -> none  [body(): gathered = lax.all_gather(kv_weight, 'fsdp', axis=0, tiled=True)]
    psum x1 -> x0, waiting for transfers between devices: 16.9 us -> none  [body(): lax.psum(shard_sum.astype(jnp.bfloat16), 'dp').astype(jnp.float32)]
    dot_general x4 -> x0, matrix products: 14 us -> none  [the longest x2 5.69 us: gradient_term(): lax.dot_general(inputs, cotangent, (((0,), (0,)), ((), ())), preferred_el...]
    slice x3 -> x0, local copies, waits for them, and re-layouts: 5.37 us -> none  [body(): gradient_term = term_from(permuted[lower:upper], flat_cot[lower:upper])]
    reshape x3 -> x0, local copies, waits for them, and re-layouts: 4.58 us -> none  [the longest x1 2.34 us: body(): input_grad = jnp.take(grad_permuted.reshape(all_rows, owners, shard_rows)...]
    gather x2 -> x0, local copies, waits for them, and re-layouts: 4.27 us -> none  [the longest x1 2.27 us: body(): jnp.take(grad_permuted.reshape(all_rows, owners, shard_rows), inverse_own...]
  transfers between devices with their start and end apart: 3 -> 0, of which waited for: 3 -> 0; matrix products, arithmetic and copies ran while one was open for 12% -> 0% of each run, Pallas kernels for 0% -> 0%
where the time goes in v1:
time: 66.4 us; the launch traced here: 66.1 us
  Pallas kernels  64 us (96%)
  local copies, waits for them, and re-layouts  1.5 us (2%)
    pallas_call x1, Pallas kernels, body(): pl.pallas_call(functools.partial(kernel, n, dp, chunk, scale), out_shape=...  56.2 us
    pallas_call x2, Pallas kernels, reorder(): pl.pallas_call(functools.partial(reorder_kernel, depth, scatter), grid=(r...  7.81 us
    unnamed x6, local copies, waits for them, and re-layouts  1.5 us

profile of v1, /device:TPU:0, one launch (start us, length us, event | category | flops | bytes accessed | tf_op | source)
XLA Modules:
  0.0 66.1 jit_solution(10021899571445705971)
XLA Ops:
  0.6 3.9 %shard_map.76.x_hbm = bf16[256,4096]{1,0:T(8,128)(2,1)} custom-call(s32[16]{0:T(128)} %order_ref.3, bf16[256,4096]{1,0:T(8,128)(2,1)} %bitcast.4), custom_call_target="tpu_custom_call" | custom-call | bytes 4194304 | tf_op jit(solution)/shard_map/pallas_call | solution.py:233
  4.5 56.2 %shard_map.77 = (bf16[256,512]{1,0:T(8,128)(2,1)}, bf16[256,4096]{1,0:T(8,128)(2,1)}, f32[256,512]{1,0:T(8,128)}) custom-call(bf16[256,4096]{1,0:T(8,128)(2,1)} %shard_map.76.x_hbm, bf16[256,512]{1,0:T(8,128)(2,1)} %bitcast.6, bf16[256,512]{1,0:T(8,128)(2,1)} %w_hbm.1, f32[256,512]{1,0:T(8,128)} %main_hbm.1), custom_call_target="tpu_custom_call" | custom-call | tf_op jit(solution)/shard_map/pallas_call | solution.py:258
  60.7 0.0 copy-start.1
  60.7 0.0 copy-start
  60.7 3.9 %shard_map.78 = bf16[256,4096]{1,0:T(8,128)(2,1)} custom-call(s32[16]{0:T(128)} %order_ref.3, bf16[256,4096]{1,0:T(8,128)(2,1)} %get-tuple-element.7.x_ref), custom_call_target="tpu_custom_call" | custom-call | bytes 4194304 | tf_op jit(solution)/shard_map/pallas_call | solution.py:233
  64.6 0.0 copy-done.1
  64.6 0.7 %copy.10 = bf16[2,128,512]{2,1,0:T(8,128)(2,1)} copy(bf16[2,128,512]{2,1,0:T(8,128)(2,1)S(1)} %bitcast.7) | data formatting | bytes 524288
  65.3 0.0 copy-done
  65.3 0.8 %copy.11 = f32[256,512]{1,0:T(8,128)} copy(f32[256,512]{1,0:T(8,128)S(1)} %copy-done) | data formatting | bytes 1048576
Async XLA Ops:
  60.7 3.9 %copy-start.1 = (bf16[256,512]{1,0:T(8,128)(2,1)S(1)}, bf16[256,512]{1,0:T(8,128)(2,1)}, u32[]{:S(2)}) copy-start(bf16[256,512]{1,0:T(8,128)(2,1)} %get-tuple-element.6) | copy-start | bytes 786436
  60.7 4.6 %copy-start = (f32[256,512]{1,0:T(8,128)S(1)}, f32[256,512]{1,0:T(8,128)}, u32[]{:S(2)}) copy-start(f32[256,512]{1,0:T(8,128)} %get-tuple-element.14) | copy-start | bytes 1572868

commit v2 on v1

--- a/solution.py
+++ b/solution.py
@@ -17,7 +17,7 @@
     n, dp, chunk, scale,
     x_hbm, c_hbm, w_hbm, main_hbm,
     key_hbm, ig_hbm, gb_hbm,
-    xx, cc, ck, gath, part, r1, t1, r2, t2, r3, fin, main, gb, key, ig,
+    xx, cc, ck, gath, part, r1, t1, r2, t2, r3, fin, main, gb, key, ig, acc,
     load_sem, out_sem, send_sem, x_recv, az_recv, a1_recv, a2_recv, ad_recv, r1_recv, r2_recv, r3_recv, rd_recv,
 ):
     f = lax.axis_index("fsdp")
@@ -108,14 +108,34 @@
     ck[...] = cc[:, :, side].reshape(2 * rows, half)
 
     per = chunk // part.shape[1]
-    for j in range(chunks):
-        both = xx[:, :, j * chunk : (j + 1) * chunk].reshape(2 * rows, chunk)
+    ring = steps + [0]
+    blockwise = per == 1
+
+    def partial(cols):
+        both = xx[:, :, cols].reshape(2 * rows, chunk)
         prod = lax.dot_general(both, ck[...], (((0,), (0,)), ((), ())), preferred_element_type=F32)
-        part[j * per : (j + 1) * per] = prod.astype(BF16).reshape(per, part.shape[1], half)
-
-    ring = steps + [0]
-    for s in ring:
-        send(part.at[peer(s) * 4 + low12], r1.at[0, peer(s)], r1_recv.at[0, peer(s)], to1)
+        return prod.astype(BF16)
+
+    def feature_block(fb):
+        return pl.ds(pl.multiple_of(fb * chunk, chunk), chunk)
+
+    def partials(lo):
+        if blockwise:
+            for s in ring:
+                fb = peer(s) * 4 + lo
+                part[fb] = partial(feature_block(fb))
+                if lo is low12:
+                    send(part.at[fb], r1.at[0, peer(s)], r1_recv.at[0, peer(s)], to1)
+                if lo is low1:
+                    send(part.at[fb], r1.at[1, peer(s)], r1_recv.at[1, peer(s)], to1)
+
+    if not blockwise:
+        for j in range(chunks):
+            made = partial(pl.ds(j * chunk, chunk))
+            part[j * per : (j + 1) * per] = made.reshape(per, part.shape[1], half)
+        for s in ring:
+            send(part.at[peer(s) * 4 + low12], r1.at[0, peer(s)], r1_recv.at[0, peer(s)], to1)
+    partials(low12)
     for s in steps:
         zb = peer(s)
         fb = zb * 4 + low
@@ -123,8 +143,51 @@
         send(block(fb), block(fb), a1_recv.at[zb], to1)
         send(block(fb), block(fb), a2_recv.at[zb], to2)
         send(block(fb), block(fb), ad_recv.at[fb], to_sib)
-    for s in ring:
-        send(part.at[peer(s) * 4 + low1], r1.at[1, peer(s)], r1_recv.at[1, peer(s)], to1)
+    if not blockwise:
+        for s in ring:
+            send(part.at[peer(s) * 4 + low1], r1.at[1, peer(s)], r1_recv.at[1, peer(s)], to1)
+    partials(low1)
+    partials(low2)
+    partials(low)
+
+    outs = []
+
+    def put(src, dst, i):
+        cp = pltpu.make_async_copy(src, dst, out_sem.at[i])
+        cp.start()
+        outs.append(cp)
+
+    contract = (((1,), (1,)), ((), ()))
+
+    def from_sib(lo):
+        for s in [0] + steps:
+            fb = peer(s) * 4 + lo
+            if s or lo is not low:
+                arrived(gath.at[1 - k, fb], ad_recv.at[fb], to_sib)
+
+    def use(lo):
+        if not blockwise:
+            return
+        from_sib(lo)
+        for s in [0] + steps:
+            fb = peer(s) * 4 + lo
+            cols = feature_block(fb)
+            w0 = gath[0, fb]
+            w1 = gath[1, fb]
+            prod = lax.dot_general(cc[0, :, :half], w0, contract, preferred_element_type=F32)
+            prod = prod + lax.dot_general(cc[0, :, half:], w1, contract, preferred_element_type=F32)
+            ig[:, cols] = prod.astype(BF16)
+            put(ig.at[:, cols], ig_hbm.at[:, cols], len(outs))
+            xb = xx[0, :, cols]
+            k0 = jnp.dot(xb, w0, preferred_element_type=F32)
+            k1 = jnp.dot(xb, w1, preferred_element_type=F32)
+            if s == 0 and lo is low:
+                acc[:, :half] = k0
+                acc[:, half:] = k1
+            else:
+                acc[:, :half] += k0
+                acc[:, half:] += k1
+
     for s in [0] + steps:
         zb = peer(s)
         fb = zb * 4 + low1
@@ -136,6 +199,7 @@
         arrived(r1.at[0, zb], r1_recv.at[0, zb], to1)
         t1[zb] = (part[zb * 4 + low2].astype(F32) + r1[0, zb].astype(F32)).astype(BF16)
         send(t1.at[zb], r2.at[zb], r2_recv.at[zb], to2)
+    use(low)
     for s in steps:
         zb = peer(s)
         arrived(r1.at[1, zb], r1_recv.at[1, zb], to1)
@@ -147,6 +211,8 @@
         fb = zb * 4 + low2
         arrived(block(fb), a2_recv.at[zb], to2)
         send(block(fb), block(fb), ad_recv.at[fb], to_sib)
+    use(low1)
+    use(low2)
     for s in [0] + steps:
         zb = peer(s)
         fb = zb * 4 + low12
@@ -163,35 +229,23 @@
     for s in range(1, dp):
         send(fin.at[d], fin.at[d], rd_recv.at[d], dev(f, lax.rem(d + s, dp)))
 
-    for s in [0] + steps:
+    use(low12)
+    if blockwise:
+        key[...] = acc[...].astype(BF16)
+    else:
         for lo in (low, low1, low2, low12):
-            if s == 0 and lo is low:
-                continue
-            fb = peer(s) * 4 + lo
-            arrived(gath.at[1 - k, fb], ad_recv.at[fb], to_sib)
-
-    outs = []
-
-    def put(src, dst, i):
-        cp = pltpu.make_async_copy(src, dst, out_sem.at[i])
-        cp.start()
-        outs.append(cp)
-
-    group = max(1, chunks // 4)
-    for j in range(chunks):
-        w0 = gath[0, j * per : (j + 1) * per].reshape(chunk, half)
-        w1 = gath[1, j * per : (j + 1) * per].reshape(chunk, half)
-        contract = (((1,), (1,)), ((), ()))
-        prod = lax.dot_general(cc[0, :, :half], w0, contract, preferred_element_type=F32)
-        prod = prod + lax.dot_general(cc[0, :, half:], w1, contract, preferred_element_type=F32)
-        ig[:, j * chunk : (j + 1) * chunk] = prod.astype(BF16)
-        if (j + 1) % group == 0:
-            cols = pl.ds((j + 1 - group) * chunk, group * chunk)
-            put(ig.at[:, cols], ig_hbm.at[:, cols], (j + 1) // group - 1)
-    for h in range(2):
-        w = gath[h].reshape(width, half)
-        key[:, h * half : (h + 1) * half] = jnp.dot(xx[0], w, preferred_element_type=F32).astype(BF16)
-    put(key, key_hbm, chunks // group)
+            from_sib(lo)
+        for j in range(chunks):
+            w0 = gath[0, j * per : (j + 1) * per].reshape(chunk, half)
+            w1 = gath[1, j * per : (j + 1) * per].reshape(chunk, half)
+            prod = lax.dot_general(cc[0, :, :half], w0, contract, preferred_element_type=F32)
+            prod = prod + lax.dot_general(cc[0, :, half:], w1, contract, preferred_element_type=F32)
+            ig[:, j * chunk : (j + 1) * chunk] = prod.astype(BF16)
+        put(ig, ig_hbm, 0)
+        for h in range(2):
+            w = gath[h].reshape(width, half)
+            key[:, h * half : (h + 1) * half] = jnp.dot(xx[0], w, preferred_element_type=F32).astype(BF16)
+    put(key, key_hbm, len(outs))
 
     for s in range(1, dp):
         src = lax.rem(d + s, dp)
@@ -203,7 +257,7 @@
             total = total + fin[2 * g + h]
         cols = slice(h * half, (h + 1) * half)
         gb[:, cols] = main[:, cols] + total * scale
-    put(gb, gb_hbm, chunks // group + 1)
+    put(gb, gb_hbm, len(outs))
     for cp in sent:
         cp.wait_send()
     for cp in outs:
@@ -249,7 +303,7 @@
     half = key_width // 2
     depth = n // 4
     scale = 1.0 / math.sqrt(rows * n * dp)
-    chunk = max(shard_rows, 256)
+    chunk = shard_rows if shard_rows % 128 == 0 else max(shard_rows, 256)
     x = reorder(normed.reshape(rows, width), owner_order, False)
     chunks = width // chunk
     dma = pltpu.SemaphoreType.DMA
@@ -280,8 +334,9 @@
             pltpu.VMEM((shard_rows, key_width), F32),
             pltpu.VMEM((rows, key_width), BF16),
             pltpu.VMEM((rows, width), BF16),
+            pltpu.VMEM((rows, key_width), F32),
             dma((5,)),
-            dma((chunks // max(1, chunks // 4) + 2,)),
+            dma((chunks + 2,)),
             dma,
             dma((2,)),
             dma((depth,)),

time: 66.4 us -> 63.8 us (0.961)
  Pallas kernels: 64 us -> 61.2 us
    pallas_call x1, Pallas kernels: 56.2 us -> 53.4 us  [body(): pl.pallas_call(functools.partial(kernel, n, dp, chunk, scale), out_shape=...]
where the time goes in v2:
time: 63.8 us; the launch traced here: 63.3 us
  Pallas kernels  61.2 us (96%)
  local copies, waits for them, and re-layouts  1.5 us (2%)
  between operations  0.66 us (1%)
    pallas_call x1, Pallas kernels, body(): pl.pallas_call(functools.partial(kernel, n, dp, chunk, scale), out_shape=...  53.4 us
    pallas_call x2, Pallas kernels, reorder(): pl.pallas_call(functools.partial(reorder_kernel, depth, scatter), grid=(r...  7.82 us
    unnamed x6, local copies, waits for them, and re-layouts  1.5 us

profile of v2, /device:TPU:0, one launch (start us, length us, event | category | flops | bytes accessed | tf_op | source)
XLA Modules:
  0.0 63.3 jit_solution(15236538689039537021)
XLA Ops:
  0.6 3.9 %shard_map.76.x_hbm = bf16[256,4096]{1,0:T(8,128)(2,1)} custom-call(s32[16]{0:T(128)} %order_ref.3, bf16[256,4096]{1,0:T(8,128)(2,1)} %bitcast.4), custom_call_target="tpu_custom_call" | custom-call | bytes 4194304 | tf_op jit(solution)/shard_map/pallas_call | solution.py:287
  4.5 53.4 %shard_map.77 = (bf16[256,512]{1,0:T(8,128)(2,1)}, bf16[256,4096]{1,0:T(8,128)(2,1)}, f32[256,512]{1,0:T(8,128)}) custom-call(bf16[256,4096]{1,0:T(8,128)(2,1)} %shard_map.76.x_hbm, bf16[256,512]{1,0:T(8,128)(2,1)} %bitcast.6, bf16[256,512]{1,0:T(8,128)(2,1)} %w_hbm.1, f32[256,512]{1,0:T(8,128)} %main_hbm.1), custom_call_target="tpu_custom_call" | custom-call | tf_op jit(solution)/shard_map/pallas_call | solution.py:312
  57.9 0.0 copy-start.1
  57.9 0.0 copy-start
  57.9 3.9 %shard_map.78 = bf16[256,4096]{1,0:T(8,128)(2,1)} custom-call(s32[16]{0:T(128)} %order_ref.3, bf16[256,4096]{1,0:T(8,128)(2,1)} %get-tuple-element.7.x_ref), custom_call_target="tpu_custom_call" | custom-call | bytes 4194304 | tf_op jit(solution)/shard_map/pallas_call | solution.py:287
  61.8 0.0 copy-done.1
  61.8 0.7 %copy.10 = bf16[2,128,512]{2,1,0:T(8,128)(2,1)} copy(bf16[2,128,512]{2,1,0:T(8,128)(2,1)S(1)} %bitcast.7) | data formatting | bytes 524288
  62.5 0.0 copy-done
  62.5 0.8 %copy.11 = f32[256,512]{1,0:T(8,128)} copy(f32[256,512]{1,0:T(8,128)S(1)} %copy-done) | data formatting | bytes 1048576
Async XLA Ops:
  57.9 4.0 %copy-start.1 = (bf16[256,512]{1,0:T(8,128)(2,1)S(1)}, bf16[256,512]{1,0:T(8,128)(2,1)}, u32[]{:S(2)}) copy-start(bf16[256,512]{1,0:T(8,128)(2,1)} %get-tuple-element.6) | copy-start | bytes 786436
  57.9 4.6 %copy-start = (f32[256,512]{1,0:T(8,128)S(1)}, f32[256,512]{1,0:T(8,128)}, u32[]{:S(2)}) copy-start(f32[256,512]{1,0:T(8,128)} %get-tuple-element.14) | copy-start | bytes 1572868
